TPU v7x, 128 devices: a whole 4x4x4 slice. The times are simulated.
128 devices in a mesh: layer: 2 (over core), px: 16 (over x, z), py: 4 (over y).
Axes of the slice: x: 4, y: 4, z: 4, core: 2. Of those that a mesh axis runs over, the one named last changes fastest.
Arguments:
- right_side: float32 [8, 2048, 4096], P('layer', 'px', 'py'), may hold values from -30 to 30
- row_conduct: float32 [8, 2048, 4096], P('layer', 'px', 'py'), may hold values from 0.5 to 2
- column_conduct: float32 [8, 2048, 4096], P('layer', 'px', 'py'), may hold values from 0.5 to 2
- via_conduct: float32 [8, 2048, 4096], P('layer', 'px', 'py'), may hold values from 0.5 to 4
- via_mask: int32 [8, 2048, 4096], P('layer', 'px', 'py'), may hold values 0 or 1
- ground_conduct: float32 [8, 2048, 4096], P('layer', 'px', 'py'), may hold values from 0.01 to 0.1
Outputs:
- solution_field: float32 [8, 2048, 4096], P('layer', 'px', 'py')
- residual: float32 [8, 2048, 4096], P('layer', 'px', 'py')
All inputs are finite; a program needn't handle non-finite values. No bound on the sum of `via_mask` on one device may be relied on, other than what follows from the above.
Results may differ from a plain program's by a relative error of at most 0.0001.
Values sent between devices are 32-bit elements; how exact they have to be, the bound alone decides.
A program may use at most 128 MiB of HBM per device.

v0:
```python
import functools

import jax
import jax.numpy as jnp
from jax import lax
from jax.experimental import pallas as pl
from jax.experimental.pallas import tpu as pltpu
from jax.sharding import PartitionSpec as P

MESH = pl.DeviceIdType.MESH
S = 8
L = 128
F32 = jnp.float32


def kernel(sizes, chunks, b_hbm, r_hbm, c_hbm, via_hbm, mask_hbm, g_hbm, bb, zb, vb, wb, ut, coef,
           rb, cb, ub, mb, gb, vm, vmask, gain, inv, mid, ef, efo, f2, f2o,
           redge, cedge, spread_c, side, colacc, row_s, row_r, col_s, col_r, pair_s, pair_r, sum_s, sum_r,
           hello_sem, load_sem, edge_sem, vm_sem, ef_sem, f2_sem, halo_sem, pair_sem, sum_sem):
    members, npx, npy = sizes
    depth, rows, width = bb.shape
    tiles = rows // S
    per = tiles // chunks
    last = depth - 1
    blocks = width // L
    up = lax.axis_index("layer")
    px = lax.axis_index("px")
    py = lax.axis_index("py")
    lower = up == 0
    lay = [k + up * (last - 2 * k) for k in range(depth)]
    via_at = [k + up * (last - 1 - 2 * k) for k in range(last)]
    chunk_rows = per * S
    peers = npx * npy
    me = px * npy + py

    partner = (1 - up, px, py)
    above, below = (up, px - 1, py), (up, px + 1, py)
    left, right = (up, px, py - 1), (up, px, py + 1)

    row_r[...] = jnp.zeros_like(row_r)
    pair_s[...] = jnp.zeros_like(pair_s)
    col_r[...] = jnp.zeros_like(col_r)
    barrier = pltpu.get_barrier_semaphore()

    deep = max(d for d in range(1, npx + 1) if npx % d == 0 and d * d <= npx)
    wide = npx // deep
    in_deep = lax.rem(px, deep)
    mates = [(up, lax.rem(px + deep * o, npx), py) for o in range(1, wide)]
    mates += [(up, px - in_deep + lax.rem(in_deep + o, deep), py) for o in range(1, deep)]
    mates += [(up, px, lax.rem(py + o, npy)) for o in range(1, npy)]
    crossing = [] if deep == 1 else [
        (jnp.logical_and(in_deep == deep - 1, px < npx - 1), below), (jnp.logical_and(in_deep == 0, px > 0), above)]

    def hello(t):
        for device in mates:
            pl.semaphore_signal(hello_sem.at[t], inc=1, device_id=device, device_id_type=MESH)

    def heard(t):
        pl.semaphore_wait(hello_sem.at[t], len(mates))

    pl.semaphore_signal(barrier, inc=1, device_id=partner, device_id_type=MESH)
    for device in mates:
        pl.semaphore_signal(barrier, inc=1, device_id=device, device_id_type=MESH)
    for exists, device in crossing:
        @pl.when(exists)
        def _():
            pl.semaphore_signal(barrier, inc=1, device_id=device, device_id_type=MESH)

    edge_loads = [
        pltpu.make_async_copy(r_hbm.at[:, pl.ds(rows - S, S)], redge, edge_sem.at[0]),
        pltpu.make_async_copy(c_hbm.at[:, :, pl.ds(width - L, L)], cedge, edge_sem.at[1]),
    ]
    for copy in edge_loads:
        copy.start()

    def chunk_at(c, ahead=0):
        start = c * chunk_rows + ahead
        return pl.ds(start if isinstance(start, int) else pl.multiple_of(start, S), chunk_rows)

    def top(c):
        at = chunk_at(c)
        return [pltpu.make_async_copy(via_hbm.at[last, at], vm.at[at], load_sem.at[c]),
                pltpu.make_async_copy(mask_hbm.at[last, at], vmask.at[at], load_sem.at[c])]

    def loads(c):
        at = chunk_at(c)
        inner = pl.ds(0, last)
        pairs = [(c_hbm.at[:, at], cb.at[:, at]),
                 (g_hbm.at[:, at], gb.at[:, at]), (via_hbm.at[inner, at], ub.at[:, at]),
                 (mask_hbm.at[inner, at], mb.at[:, at]), (b_hbm.at[:, at], bb.at[:, at])]
        return [pltpu.make_async_copy(src, dst, load_sem.at[c]) for src, dst in pairs]

    def row_load(c):
        start = c * chunk_rows - (S if c == 1 else 0)
        size = chunk_rows + (S if c == 1 else -S if c == 0 else 0)
        return pltpu.make_async_copy(
            r_hbm.at[:, pl.ds(start, size)], rb.at[:, pl.ds(start + S, size)], load_sem.at[c])

    def start_loads(c):
        row_load(c).start()
        for copy in loads(c):
            copy.start()

        @pl.when(lower)
        def _():
            for copy in top(c):
                copy.start()

    start_loads(1 % chunks)

    lane = lax.broadcasted_iota(jnp.int32, (S, L), 1)
    sub = lax.broadcasted_iota(jnp.int32, (S, L), 0)
    first_lane, final_lane = lane == 0, lane == L - 1
    first_sub, final_sub = sub == 0, sub == S - 1

    def remote(src, dst, sems, device):
        return pltpu.make_async_remote_copy(
            src_ref=src, dst_ref=dst, send_sem=sems.at[0], recv_sem=sems.at[1],
            device_id=device, device_id_type=MESH)

    def exchanges(trip):
        def one(e, src, dst, device):
            return remote(src, dst, halo_sem.at[trip % 2, e], device)

        down_up = [
            (px < npx - 1, px > 0, one(0, row_s.at[trip, 0], row_r.at[trip, 0], below)),
            (px > 0, px < npx - 1, one(1, row_s.at[trip, 1], row_r.at[trip, 1], above)),
        ]
        for part in range(2):
            sent, got = col_s.at[trip, part], col_r.at[trip, part]
            down_up.append((py < npy - 1, py > 0, one(2 + 2 * part, sent.at[0], got.at[0], right)))
            down_up.append((py > 0, py < npy - 1, one(3 + 2 * part, sent.at[1], got.at[1], left)))
        return down_up

    def send_halo(trip, which):
        for e in which:
            sends, _, copy = exchanges(trip)[e]
            pl.when(sends)(copy.start)

    def take_halo(trip, which):
        for e in which:
            sends, takes, copy = exchanges(trip)[e]
            pl.when(takes)(copy.wait_recv)

    def end_halo(trip, which):
        for e in which:
            sends, _, copy = exchanges(trip)[e]
            pl.when(sends)(copy.wait_send)

    for copy in edge_loads:
        copy.wait()
    for c in range(1, chunks):
        start_loads((1 + c) % chunks)
    for k in range(depth):
        row_s[0, 0, k:k + 1, :] = redge[lay[k], S - 1:S, :]
        acc = jnp.zeros((S, L), F32)
        for i in range(tiles):
            edge = jnp.broadcast_to(cedge[lay[k], i * S:(i + 1) * S, L - 1:L], (S, L))
            acc = jnp.where(lane == sub + i * S, edge, acc)
        col_s[0, 0, 0, k:k + 1, :] = jnp.sum(acc, axis=0, keepdims=True)

    pl.semaphore_wait(barrier, 1 + len(mates) + sum(exists.astype(jnp.int32) for exists, _ in crossing))
    send_halo(0, (0, 2))
    hello(0)
    take_halo(0, (2,))

    def spread(ref):
        for k in range(depth):
            both = jnp.concatenate([jnp.broadcast_to(ref[side_of, k:k + 1, :], (L // 2, L)) for side_of in range(2)], axis=0)
            spread_c[k] = jnp.transpose(both)[:rows]

    def rows_at(i):
        return pl.ds(pl.multiple_of(i * S, S), S)

    def cut(j):
        return pl.ds(j * L, L)

    def next_row(now, after):
        return pltpu.roll(jnp.where(first_sub, after, now), S - 1, 0)

    def prev_row(now, before):
        return pltpu.roll(jnp.where(final_sub, before, now), 1, 0)

    def from_left(parts, edge):
        turned = [pltpu.roll(p, 1, 1) for p in parts]
        return [jnp.where(first_lane, turned[j - 1] if j else edge, turned[j]) for j in range(blocks)]

    def factor_tile(i):
        at, pad = rows_at(i), rows_at(i + 1)
        coupling, g, y = [None] * blocks, [None] * blocks, [None] * blocks
        for k in range(depth):
            edge = spread_c[k, at, :]
            c = [cb[lay[k], at, cut(j)] for j in range(blocks)]
            c_left = from_left(c, edge)
            for j in range(blocks):
                r = rb[lay[k], pad, cut(j)]
                d = gb[lay[k], at, cut(j)] + r + prev_row(r, rb[lay[k], at, cut(j)]) + c[j] + c_left[j]
                rhs = bb[lay[k], at, cut(j)]
                if k:
                    d = d + coupling[j] - coupling[j] * g[j]
                    rhs = rhs + g[j] * y[j]
                y[j] = rhs
                if k < last:
                    coupling[j] = ub[via_at[k], at, cut(j)] * mb[via_at[k], at, cut(j)].astype(F32)
                    inverse = 1.0 / (d + coupling[j])
                    g[j] = coupling[j] * inverse
                    gain[k, at, cut(j)] = g[j]
                    inv[k, at, cut(j)] = inverse
                    zb[lay[k], pad, cut(j)] = rhs * inverse
                else:
                    ef[0, at, cut(j)] = d
                    ef[1, at, cut(j)] = rhs

    def to_partner(src, dst, sems, c):
        return pltpu.make_async_remote_copy(
            src_ref=src, dst_ref=dst, send_sem=sems.at[chunks], recv_sem=sems.at[c],
            device_id=partner, device_id_type=MESH)

    def all_sent(ref, sems):
        pltpu.make_async_copy(ref, ref, sems.at[chunks]).wait()

    def vm_copy(c):
        return to_partner(vm.at[chunk_at(c)], vm.at[chunk_at(c)], vm_sem, c)

    def ef_copy(c):
        return to_partner(ef.at[:, chunk_at(c)], efo.at[:, chunk_at(c)], ef_sem, c)

    def f2_copy(c):
        return to_partner(f2.at[chunk_at(c)], f2o.at[chunk_at(c)], f2_sem, c)

    def low_last(q):
        return lax.rem(q + 1, chunks)

    def high_last(q):
        return jnp.where(q < chunks - 2, q + 1, jnp.where(q == chunks - 2, 0, chunks - 1))

    def in_chunks(tile, order=low_last, before=None, after=None):
        def chunk(q, _):
            c = order(q)
            if before is not None:
                before(c)

            def one(j, _):
                tile(c * per + j)
                return 0

            lax.fori_loop(0, per, one, 0)
            if after is not None:
                after(c)
            return 0

        lax.fori_loop(0, chunks, chunk, 0)

    def wait_loads(c):
        for one in range(chunks):
            pl.when(c == one)(row_load(one).wait)
        for copy in loads(c):
            copy.wait()

        @pl.when(c == 0)
        def _():
            take_halo(0, (0,))
            for k in range(depth):
                rb[lay[k], S - 1:S, :] = row_r[0, 0, k:k + 1, :]

        @pl.when(lower)
        def _():
            for copy in top(c):
                copy.wait()

        @pl.when(lower)
        def _():
            def times(j, _):
                at = rows_at(c * per + j)
                for b in range(blocks):
                    vm[at, cut(b)] = vm[at, cut(b)] * vmask[at, cut(b)].astype(F32)
                return 0

            lax.fori_loop(0, per, times, 0)
            vm_copy(c).start()

    spread(col_r.at[0, 0])
    in_chunks(factor_tile, before=wait_loads, after=lambda c: ef_copy(c).start())

    def back(field, i, own):
        at, pad = rows_at(i), rows_at(i + 1)
        mine = lane == sub + i * S
        value = own
        for k in range(last, -1, -1):
            for j in range(blocks):
                if k < last:
                    value[j] = field[lay[k], pad, cut(j)] + gain[k, at, cut(j)] * value[j]
                field[lay[k], pad, cut(j)] = value[j]
            first = jnp.broadcast_to(value[0][:, 0:1], (S, L))
            final = jnp.broadcast_to(value[blocks - 1][:, L - 1:L], (S, L))
            colacc[0, k] = jnp.where(mine, final, colacc[0, k])
            colacc[1, k] = jnp.where(mine, first, colacc[1, k])

    def back_first(i):
        at = rows_at(i)
        value = []
        for j in range(blocks):
            e, f = ef[0, at, cut(j)], ef[1, at, cut(j)]
            eo, fo = efo[0, at, cut(j)], efo[1, at, cut(j)]
            v = vm[at, cut(j)]
            shared = 1.0 / (e * eo + v * (e + eo))
            own, cross = (eo + v) * shared, v * shared
            mid[0, at, cut(j)] = own
            mid[1, at, cut(j)] = cross
            value.append(own * f + cross * fo)
        back(zb, i, value)

    def back_second(i):
        at = rows_at(i)
        back(vb, i, [mid[0, at, cut(j)] * f2[at, cut(j)] + mid[1, at, cut(j)] * f2o[at, cut(j)] for j in range(blocks)])

    def send_part(field, trip, part, side_of):
        at = S if side_of else rows + S - 1
        for k in range(depth):
            row_s[trip, side_of, k:k + 1, :] = field[lay[k], at:at + 1, :]
            final = jnp.sum(colacc[0, k], axis=0, keepdims=True)
            col_s[trip, part, 0, k:k + 1, :] = final * col_s[0, 0, 0, k:k + 1, :]
            col_s[trip, part, 1, k:k + 1, :] = jnp.sum(colacc[1, k], axis=0, keepdims=True)
        send_halo(trip, (side_of, 2 + 2 * part, 3 + 2 * part))

    def receive_row(field, trip, side_of):
        at = rows + S if side_of else S - 1
        take_halo(trip, (side_of,))
        for k in range(depth):
            field[lay[k], at:at + 1, :] = row_r[trip, side_of, k:k + 1, :]

    def low_tiles(p):
        return jnp.where(p < tiles - per - 1, p + per, jnp.where(p < tiles - 1, tiles - 2 - p, tiles - 1))

    def high_tiles(p):
        return lax.rem(p + 1, tiles)

    def sideways(field, i, k):
        at, pad, ahead = rows_at(i), rows_at(i + 1), rows_at(i + 2)
        value = [field[lay[k], pad, cut(j)] for j in range(blocks)]
        c = [cb[lay[k], at, cut(j)] for j in range(blocks)]
        outside = spread_c[k, at, :]
        turned = [(pltpu.roll(c[j] * value[j], 1, 1), pltpu.roll(value[j], L - 1, 1)) for j in range(blocks)]
        to_right = [jnp.where(first_lane, turned[j - 1][0] if j else outside, turned[j][0]) for j in range(blocks)]
        beside = [jnp.where(final_lane, turned[j + 1][1] if j < blocks - 1 else outside, turned[j][1])
                  for j in range(blocks)]
        for j in range(blocks):
            r = rb[lay[k], pad, cut(j)]
            down = r * value[j]
            before = rb[lay[k], at, cut(j)] * field[lay[k], at, cut(j)]
            term = r * next_row(value[j], field[lay[k], ahead, cut(j)]) + prev_row(down, before)
            side[k, :, cut(j)] = term + (c[j] * beside[j] + to_right[j])

    def first_sides(field, trip):
        take_halo(trip, (2, 3))
        spread(col_r.at[trip, 0])
        for k in range(depth):
            sideways(field, per if trip == 1 else 1, k)

    def take_columns(trip):
        take_halo(trip, (4, 5))
        spread(col_r.at[trip, 1])

    def images(field, trip, order, begin, carry, after=None):
        needs = [(tiles - per - 1, lambda: take_columns(trip)),
                 (tiles - 2 if trip == 1 else tiles - 1, lambda: receive_row(field, trip, 0)),
                 (tiles - 1 if trip == 1 else tiles - 2, lambda: receive_row(field, trip, 1))]

        def chunk(q, carry):
            for j in range(per):
                for place, take in needs:
                    if (place - 1) % per == j:
                        pl.when(q == (place - 1) // per)(take)
                position = q * per + j
                use, ahead = begin(order(position)), order(lax.rem(position + 1, tiles))
                for k in range(depth):
                    carry = use(k, [side[k, :, cut(b)] for b in range(blocks)], carry)
                    sideways(field, ahead, k)
            if after is not None:
                after(q)
            return carry

        return lax.fori_loop(0, chunks, chunk, carry)

    def down(total):
        return jnp.sum(total, axis=0, keepdims=True)

    def across(total):
        return jnp.sum(total, axis=1, keepdims=True)

    def pair_copy(slot):
        return remote(pair_s.at[slot], pair_r.at[slot], pair_sem.at[slot], partner)

    def pair_begin(slot, totals):
        for q, total in enumerate(totals):
            pair_s[slot, q:q + 1, :] = down(total)
        pair_copy(slot).start()

    def pair_finish(slot):
        pair_copy(slot).wait_recv()
        return across(pair_s[slot] + pair_r[slot])

    def sum_copies():
        def way(o, n):
            return min(o, n - o)

        offsets = [(a, b) for a in range(npx) for b in range(npy) if a or b]
        offsets.sort(key=lambda o: -way(o[0] // deep, wide) - way(o[0] % deep, deep) - way(o[1], npy))
        to_x, to_y = [lax.rem(px + a, npx) for a in range(npx)], [lax.rem(py + b, npy) for b in range(npy)]
        return [remote(sum_s, sum_r.at[me], sum_sem, (up, to_x[a], to_y[b])) for a, b in offsets]

    def sum_bytes(end):
        part = sum_r.at[pl.ds(0, peers - 1)]
        return pltpu.make_async_copy(part, part, sum_sem.at[end])

    colacc[...] = jnp.zeros_like(colacc)

    def wait_middle(c):
        ef_copy(c).wait_recv()
        pl.when(up == 1)(vm_copy(c).wait_recv)

    in_chunks(back_first, before=wait_middle,
              after=lambda c: pl.when(c == chunks - 1)(lambda: send_part(zb, 1, 0, 0)))
    send_part(zb, 1, 1, 1)
    heard(0)
    hello(1)

    zero = jnp.zeros((S, L), F32)

    def image_first(i):
        at, pad = rows_at(i), rows_at(i + 1)
        y = [None] * blocks

        def use(k, terms, sums):
            one, two = sums
            for j in range(blocks):
                b, value = bb[lay[k], at, cut(j)], zb[lay[k], pad, cut(j)]
                w = b - terms[j]
                wb[lay[k], at, cut(j)] = w
                one = one + b * value
                two = two + w * value
                y[j] = w if k == 0 else w + gain[k - 1, at, cut(j)] * y[j]
                if k < last:
                    vb[lay[k], pad, cut(j)] = y[j] * inv[k, at, cut(j)]
                else:
                    f2[at, cut(j)] = y[j]
            return one, two

        return use

    first_sides(zb, 1)
    one, two = images(zb, 1, low_tiles, image_first, (zero, zero),
                      after=lambda q: pl.when(q < chunks - 2)(lambda: f2_copy(q + 1).start()))
    f2_copy(0).start()
    f2_copy(chunks - 1).start()
    pair_begin(0, (one, two))
    end_halo(0, (0, 2))
    in_chunks(back_second, order=high_last, before=lambda c: f2_copy(c).wait_recv(),
              after=lambda c: pl.when(c == 0)(lambda: send_part(vb, 2, 0, 1)))
    send_part(vb, 2, 1, 0)
    here = pair_finish(0)
    rho_here, power_here = here[0:1], here[1:2]
    known = power_here > 0.0
    guess = jnp.where(known, jnp.clip(rho_here / jnp.where(known, power_here, 1.0), 0.25, 256.0), 1.0)
    step = jnp.broadcast_to(guess, (S, L))
    first_sides(vb, 2)

    def image_second(i):
        at, pad = rows_at(i), rows_at(i + 1)

        def use(k, terms, sums):
            rp, wv, qp, uv, uz = sums
            for j in range(blocks):
                w, v, z = wb[lay[k], at, cut(j)], vb[lay[k], pad, cut(j)], zb[lay[k], pad, cut(j)]
                u = w - terms[j]
                ut[lay[k], at, cut(j)] = u
                p = z - step * v
                rp = rp + (bb[lay[k], at, cut(j)] - step * w) * p
                wv = wv + w * v
                qp = qp + (w - step * u) * p
                uv = uv + u * v
                uz = uz + u * z
            return rp, wv, qp, uv, uz

        return use

    sums = images(vb, 2, high_tiles, image_second, (zero,) * 5)
    pair_begin(1, sums)
    heard(1)
    here = pair_finish(1)
    rp, wv, qp, uv, uz = [here[q:q + 1] for q in range(5)]
    entries = [rp, qp, power_here - guess * wv, 0.5 * (wv + uz) - guess * uv, wv, uv, guess, guess, rho_here, power_here]
    row = jnp.zeros((1, L), F32)
    for q, entry in enumerate(entries):
        row = jnp.where(lane[0:1] == q, entry, row)
    sum_s[...] = row
    sum_r[me] = row

    for copy in sum_copies():
        copy.start()

    end_halo(1, range(6))
    end_halo(2, range(6))
    all_sent(ef, ef_sem)
    all_sent(f2, f2_sem)
    pl.when(lower)(lambda: all_sent(vm, vm_sem))
    pair_copy(0).wait_send()
    pair_copy(1).wait_send()

    def pick(total, q):
        return across(jnp.where(lane[0:1] == q, total, 0.0))

    sum_bytes(1).wait()
    rows_all = sum_r[...].reshape(peers, L)
    total = down(rows_all)
    rho = pick(total, 8)
    alpha = rho / pick(total, 9)
    off = alpha - pltpu.roll(rows_all, L - 6, 1)
    total = down(rows_all - off * (2.0 * pltpu.roll(rows_all, L - 2, 1) - off * pltpu.roll(rows_all, L - 4, 1)))
    rho_next, curvature = pick(total, 0), pick(total, 1)
    ratio = rho_next / rho
    beta = rho_next / (curvature - ratio * rho_next / alpha)
    coef[0] = jnp.broadcast_to(alpha + beta * (1.0 + ratio), (S, L))
    coef[1] = jnp.broadcast_to(beta * alpha, (S, L))

    sum_bytes(0).wait()


def finish(chunks, bb, zb, vb, wb, ut, coef, x_hbm, res_hbm, xb, resb, out_sem):
    depth, rows, width = bb.shape
    chunk_rows = rows // chunks
    on_z, on_v = coef[0], coef[1]

    def out_copies(c):
        at = pl.ds(c * chunk_rows, chunk_rows)
        return [pltpu.make_async_copy(xb.at[:, at], x_hbm.at[:, at], out_sem.at[0, c]),
                pltpu.make_async_copy(resb.at[:, at], res_hbm.at[:, at], out_sem.at[1, c])]

    for c in range(chunks):
        def tile(t, _):
            start = pl.multiple_of(c * chunk_rows + t * S, S)
            at, pad = pl.ds(start, S), pl.ds(pl.multiple_of(start + S, S), S)
            for k in range(depth):
                for j in range(width // L):
                    cut = pl.ds(j * L, L)
                    xb[k, at, cut] = on_z * zb[k, pad, cut] - on_v * vb[k, pad, cut]
                    resb[k, at, cut] = bb[k, at, cut] - on_z * wb[k, at, cut] + on_v * ut[k, at, cut]
            return 0

        lax.fori_loop(0, chunk_rows // S, tile, 0)
        for copy in out_copies(c):
            copy.start()
    for c in range(chunks):
        for copy in out_copies(c):
            copy.wait()


def solution(mesh):
    sizes = tuple(mesh.shape[name] for name in ("layer", "px", "py"))
    members, npx, npy = sizes
    assert members == 2

    def shards(*arrays):
        depth, rows, width = arrays[0].shape
        assert rows <= L and rows % S == 0 and width % L == 0 and depth >= 2
        chunks = max(c for c in (2, 4) if (rows // S) % c == 0)
        peers = npx * npy
        full, plane, inner = (depth, rows, width), (rows, width), (depth - 1, rows, width)
        padded = (depth, rows + 2 * S, width)
        dma = pltpu.SemaphoreType.DMA

        def vmem(*shape, dtype=F32):
            return pltpu.VMEM(shape, dtype)

        scratch = [
            vmem(depth, rows + S, width), vmem(*full), vmem(*inner), vmem(*inner, dtype=jnp.int32), vmem(*full),
            vmem(*plane), vmem(*plane, dtype=jnp.int32),
            vmem(*inner), vmem(*inner), vmem(2, *plane), vmem(2, *plane), vmem(2, *plane), vmem(*plane), vmem(*plane),
            vmem(depth, S, width), vmem(depth, rows, L), vmem(depth, rows, L), vmem(depth, S, width), vmem(2, depth, S, L),
            vmem(3, 2, depth, width), vmem(3, 2, depth, width), vmem(3, 2, 2, depth, L), vmem(3, 2, 2, depth, L),
            vmem(2, S, L), vmem(2, S, L), vmem(1, L), vmem(peers, 1, L),
            pltpu.SemaphoreType.REGULAR((2,)),
            dma((chunks,)), dma((2,)), dma((chunks + 1,)), dma((chunks + 1,)), dma((chunks + 1,)), dma((2, 6, 2)),
            dma((2, 2)), dma((2,)),
        ]
        anywhere = pl.BlockSpec(memory_space=pl.ANY)
        kept = pl.pallas_call(
            functools.partial(kernel, sizes, chunks),
            out_shape=(vmem(*full), vmem(*padded), vmem(*padded), vmem(*full), vmem(*full), vmem(2, S, L)),
            in_specs=[anywhere] * 6,
            out_specs=(pl.BlockSpec(memory_space=pltpu.VMEM),) * 6,
            scratch_shapes=scratch,
            compiler_params=pltpu.CompilerParams(
                collective_id=0, has_side_effects=True, vmem_limit_bytes=52 * 1024 * 1024),
            name="pcg",
        )(*arrays)
        return pl.pallas_call(
            functools.partial(finish, chunks),
            out_shape=(jax.ShapeDtypeStruct(full, F32), jax.ShapeDtypeStruct(full, F32)),
            in_specs=[pl.BlockSpec(memory_space=pltpu.VMEM)] * 6,
            out_specs=(anywhere,) * 2,
            scratch_shapes=[vmem(*full), vmem(*full), dma((2, chunks))],
            compiler_params=pltpu.CompilerParams(vmem_limit_bytes=8 * 1024 * 1024),
            name="finish",
        )(*kept)

    spec = P("layer", "px", "py")
    return jax.shard_map(shards, mesh=mesh, in_specs=(spec,) * 6, out_specs=(spec, spec), check_vma=False)
```

profile of v0, /device:TPU:1, one launch (start us, length us, event | category | flops | bytes accessed | tf_op | source)
XLA Modules:
  0.0 35.5 jit_solution(5773899474425364546)
XLA Ops:
  0.6 32.7 %pcg.1 = (f32[4,128,1024]{2,1,0:T(8,128)S(1)}, f32[4,144,1024]{2,1,0:T(8,128)S(1)}, f32[4,144,1024]{2,1,0:T(8,128)S(1)}, f32[4,128,1024]{2,1,0:T(8,128)S(1)}, f3...) custom-call(f32[4,128,1024]{2,1,0:T(8,128)} %b_hbm.1, f32[4,128,1024]{2,1,0:T(8,128)} %r_hbm.1, ...), custom_call_target="tpu_custom_call" | custom-call | tf_op jit(solution)/shard_map/pcg/pallas_call | solution.py:587
  33.3 2.2 %finish.1 = (f32[4,128,1024]{2,1,0:T(8,128)}, f32[4,128,1024]{2,1,0:T(8,128)}) custom-call(f32[4,128,1024]{2,1,0:T(8,128)S(1)} %get-tuple-element.8.bb, f32[4,144,1024]{2,1,0:T(8,128)S(1)} %get-tuple-element.9.zb, f32[4,144,1024]{2,1,0:T(8,128)S(1)} %get-tuple-element.10.vb, f32[4,128,1024]{2,1,0:T(8,128)S(1)} %get-tuple-element.11.wb, ...), custom_call_target="tpu_custom_call" | custom-call | tf_op jit(solution)/shard_map/finish/pallas_call | solution.py:597
where the time goes:
time: 35.7 us; the launch traced here: 35.5 us
  Pallas kernels  34.9 us (98%)
  between operations  0.64 us (2%)
    pallas_call x1, Pallas kernels, shards(): pl.pallas_call(functools.partial(kernel, sizes, chunks), out_shape=(vmem(...  32.7 us
    pallas_call x1, Pallas kernels, shards(): pl.pallas_call(functools.partial(finish, chunks), out_shape=(jax.ShapeDty...  2.22 us

commit v1 on v0

--- a/solution.py
+++ b/solution.py
@@ -45,26 +45,50 @@
     deep = max(d for d in range(1, npx + 1) if npx % d == 0 and d * d <= npx)
     wide = npx // deep
     in_deep = lax.rem(px, deep)
-    mates = [(up, lax.rem(px + deep * o, npx), py) for o in range(1, wide)]
-    mates += [(up, px - in_deep + lax.rem(in_deep + o, deep), py) for o in range(1, deep)]
-    mates += [(up, px, lax.rem(py + o, npy)) for o in range(1, npy)]
+    across_wide = [(up, lax.rem(px + deep * o, npx), py) for o in range(1, wide)]
+    along_deep = [(up, px - in_deep + lax.rem(in_deep + o, deep), py) for o in range(1, deep)]
+    along_py = [(up, px, lax.rem(py + o, npy)) for o in range(1, npy)]
+    mates = [(None, device) for device in across_wide + along_deep + along_py]
+
+    def within(reach):
+        found = []
+        for o in [o for r in range(1, reach + 1) for o in (-r, r)]:
+            if abs(o) < deep:
+                found.append((jnp.logical_and(in_deep + o >= 0, in_deep + o < deep), (up, px + o, py)))
+            if abs(o) < npy:
+                found.append((jnp.logical_and(py + o >= 0, py + o < npy), (up, px, py + o)))
+        return found
+
     crossing = [] if deep == 1 else [
         (jnp.logical_and(in_deep == deep - 1, px < npx - 1), below), (jnp.logical_and(in_deep == 0, px > 0), above)]
+    near = [(None, partner)] + [(None, device) for device in across_wide] + within(1) + crossing
+    rounds, reach = [], 1
+    while reach < max(deep, npy) - 1:
+        rounds.append(within(reach))
+        reach *= 2
+    rounds += [mates, mates]
+    assert len(rounds) <= hello_sem.shape[0]
+
+    def greet(sem, targets):
+        for exists, device in targets:
+            def signal(device=device):
+                pl.semaphore_signal(sem, inc=1, device_id=device, device_id_type=MESH)
+
+            signal() if exists is None else pl.when(exists)(signal)
+
+    def count(targets):
+        return sum(1 if exists is None else exists.astype(jnp.int32) for exists, _ in targets)
 
     def hello(t):
-        for device in mates:
-            pl.semaphore_signal(hello_sem.at[t], inc=1, device_id=device, device_id_type=MESH)
+        greet(hello_sem.at[t], rounds[t])
 
     def heard(t):
-        pl.semaphore_wait(hello_sem.at[t], len(mates))
-
-    pl.semaphore_signal(barrier, inc=1, device_id=partner, device_id_type=MESH)
-    for device in mates:
-        pl.semaphore_signal(barrier, inc=1, device_id=device, device_id_type=MESH)
-    for exists, device in crossing:
-        @pl.when(exists)
-        def _():
-            pl.semaphore_signal(barrier, inc=1, device_id=device, device_id_type=MESH)
+        if t < len(rounds):
+            pl.semaphore_wait(hello_sem.at[t], count(rounds[t]))
+        if t + 1 < len(rounds):
+            hello(t + 1)
+
+    greet(barrier, near)
 
     edge_loads = [
         pltpu.make_async_copy(r_hbm.at[:, pl.ds(rows - S, S)], redge, edge_sem.at[0]),
@@ -120,7 +144,9 @@
 
     def exchanges(trip):
         def one(e, src, dst, device):
-            return remote(src, dst, halo_sem.at[trip % 2, e], device)
+            return pltpu.make_async_remote_copy(
+                src_ref=src, dst_ref=dst, send_sem=halo_sem.at[2, 0], recv_sem=halo_sem.at[trip % 2, e],
+                device_id=device, device_id_type=MESH)
 
         down_up = [
             (px < npx - 1, px > 0, one(0, row_s.at[trip, 0], row_r.at[trip, 0], below)),
@@ -159,7 +185,7 @@
             acc = jnp.where(lane == sub + i * S, edge, acc)
         col_s[0, 0, 0, k:k + 1, :] = jnp.sum(acc, axis=0, keepdims=True)
 
-    pl.semaphore_wait(barrier, 1 + len(mates) + sum(exists.astype(jnp.int32) for exists, _ in crossing))
+    pl.semaphore_wait(barrier, count(near))
     send_halo(0, (0, 2))
     hello(0)
     take_halo(0, (2,))
@@ -335,11 +361,11 @@
     def high_tiles(p):
         return lax.rem(p + 1, tiles)
 
-    def sideways(field, i, k):
+    def sideways(field, i, k, outside=None):
         at, pad, ahead = rows_at(i), rows_at(i + 1), rows_at(i + 2)
         value = [field[lay[k], pad, cut(j)] for j in range(blocks)]
         c = [cb[lay[k], at, cut(j)] for j in range(blocks)]
-        outside = spread_c[k, at, :]
+        outside = spread_c[k, at, :] if outside is None else outside
         turned = [(pltpu.roll(c[j] * value[j], 1, 1), pltpu.roll(value[j], L - 1, 1)) for j in range(blocks)]
         to_right = [jnp.where(first_lane, turned[j - 1][0] if j else outside, turned[j][0]) for j in range(blocks)]
         beside = [jnp.where(final_lane, turned[j + 1][1] if j < blocks - 1 else outside, turned[j][1])
@@ -352,10 +378,16 @@
             side[k, :, cut(j)] = term + (c[j] * beside[j] + to_right[j])
 
     def first_sides(field, trip):
+        i = per if trip == 1 else 1
+        at, end = pl.ds(i * S, S), cut(blocks - 1)
+        for k in range(depth):
+            sideways(field, i, k, jnp.zeros((S, L), F32))
         take_halo(trip, (2, 3))
         spread(col_r.at[trip, 0])
         for k in range(depth):
-            sideways(field, per if trip == 1 else 1, k)
+            outside = spread_c[k, at, :]
+            side[k, :, cut(0)] += jnp.where(first_lane, outside, 0.0)
+            side[k, :, end] += cb[lay[k], at, end] * jnp.where(final_lane, outside, 0.0)
 
     def take_columns(trip):
         take_halo(trip, (4, 5))
@@ -413,6 +445,7 @@
         part = sum_r.at[pl.ds(0, peers - 1)]
         return pltpu.make_async_copy(part, part, sum_sem.at[end])
 
+    heard(0)
     colacc[...] = jnp.zeros_like(colacc)
 
     def wait_middle(c):
@@ -422,8 +455,6 @@
     in_chunks(back_first, before=wait_middle,
               after=lambda c: pl.when(c == chunks - 1)(lambda: send_part(zb, 1, 0, 0)))
     send_part(zb, 1, 1, 1)
-    heard(0)
-    hello(1)
 
     zero = jnp.zeros((S, L), F32)
 
@@ -449,15 +480,16 @@
         return use
 
     first_sides(zb, 1)
+    heard(1)
     one, two = images(zb, 1, low_tiles, image_first, (zero, zero),
                       after=lambda q: pl.when(q < chunks - 2)(lambda: f2_copy(q + 1).start()))
     f2_copy(0).start()
     f2_copy(chunks - 1).start()
     pair_begin(0, (one, two))
-    end_halo(0, (0, 2))
     in_chunks(back_second, order=high_last, before=lambda c: f2_copy(c).wait_recv(),
               after=lambda c: pl.when(c == 0)(lambda: send_part(vb, 2, 0, 1)))
     send_part(vb, 2, 1, 0)
+    heard(2)
     here = pair_finish(0)
     rho_here, power_here = here[0:1], here[1:2]
     known = power_here > 0.0
@@ -486,7 +518,8 @@
 
     sums = images(vb, 2, high_tiles, image_second, (zero,) * 5)
     pair_begin(1, sums)
-    heard(1)
+    for t in range(3, len(rounds)):
+        heard(t)
     here = pair_finish(1)
     rp, wv, qp, uv, uz = [here[q:q + 1] for q in range(5)]
     entries = [rp, qp, power_here - guess * wv, 0.5 * (wv + uz) - guess * uv, wv, uv, guess, guess, rho_here, power_here]
@@ -499,6 +532,7 @@
     for copy in sum_copies():
         copy.start()
 
+    end_halo(0, (0, 2))
     end_halo(1, range(6))
     end_halo(2, range(6))
     all_sent(ef, ef_sem)
@@ -531,10 +565,9 @@
     chunk_rows = rows // chunks
     on_z, on_v = coef[0], coef[1]
 
-    def out_copies(c):
-        at = pl.ds(c * chunk_rows, chunk_rows)
-        return [pltpu.make_async_copy(xb.at[:, at], x_hbm.at[:, at], out_sem.at[0, c]),
-                pltpu.make_async_copy(resb.at[:, at], res_hbm.at[:, at], out_sem.at[1, c])]
+    def out_copies(at):
+        return [pltpu.make_async_copy(xb.at[:, at], x_hbm.at[:, at], out_sem.at[0]),
+                pltpu.make_async_copy(resb.at[:, at], res_hbm.at[:, at], out_sem.at[1])]
 
     for c in range(chunks):
         def tile(t, _):
@@ -548,11 +581,10 @@
             return 0
 
         lax.fori_loop(0, chunk_rows // S, tile, 0)
-        for copy in out_copies(c):
+        for copy in out_copies(pl.ds(c * chunk_rows, chunk_rows)):
             copy.start()
-    for c in range(chunks):
-        for copy in out_copies(c):
-            copy.wait()
+    for copy in out_copies(pl.ds(0, rows)):
+        copy.wait()
 
 
 def solution(mesh):
@@ -579,8 +611,8 @@
             vmem(depth, S, width), vmem(depth, rows, L), vmem(depth, rows, L), vmem(depth, S, width), vmem(2, depth, S, L),
             vmem(3, 2, depth, width), vmem(3, 2, depth, width), vmem(3, 2, 2, depth, L), vmem(3, 2, 2, depth, L),
             vmem(2, S, L), vmem(2, S, L), vmem(1, L), vmem(peers, 1, L),
-            pltpu.SemaphoreType.REGULAR((2,)),
-            dma((chunks,)), dma((2,)), dma((chunks + 1,)), dma((chunks + 1,)), dma((chunks + 1,)), dma((2, 6, 2)),
+            pltpu.SemaphoreType.REGULAR((4,)),
+            dma((chunks,)), dma((2,)), dma((chunks + 1,)), dma((chunks + 1,)), dma((chunks + 1,)), dma((3, 6)),
             dma((2, 2)), dma((2,)),
         ]
         anywhere = pl.BlockSpec(memory_space=pl.ANY)
@@ -595,11 +627,11 @@
             name="pcg",
         )(*arrays)
         return pl.pallas_call(
-            functools.partial(finish, chunks),
+            functools.partial(finish, 2 * chunks if rows % (2 * chunks * S) == 0 else chunks),
             out_shape=(jax.ShapeDtypeStruct(full, F32), jax.ShapeDtypeStruct(full, F32)),
             in_specs=[pl.BlockSpec(memory_space=pltpu.VMEM)] * 6,
             out_specs=(anywhere,) * 2,
-            scratch_shapes=[vmem(*full), vmem(*full), dma((2, chunks))],
+            scratch_shapes=[vmem(*full), vmem(*full), dma((2,))],
             compiler_params=pltpu.CompilerParams(vmem_limit_bytes=8 * 1024 * 1024),
             name="finish",
         )(*kept)

time: 35.7 us -> 35.5 us (level)
  no operation moved by 1% of the time
where the time goes in v1:
time: 35.5 us; the launch traced here: 35.3 us
  Pallas kernels  34.7 us (98%)
  between operations  0.64 us (2%)
    pallas_call x1, Pallas kernels, shards(): pl.pallas_call(functools.partial(kernel, sizes, chunks), out_shape=(vmem(...  32.6 us
    pallas_call x1, Pallas kernels, shards(): pl.pallas_call(functools.partial(finish, 2 * chunks if rows % (2 * chunks...  2.08 us

profile of v1, /device:TPU:1, one launch (start us, length us, event | category | flops | bytes accessed | tf_op | source)
XLA Modules:
  0.0 35.3 jit_solution(6756965783152110053)
XLA Ops:
  0.6 32.6 %pcg.1 = (f32[4,128,1024]{2,1,0:T(8,128)S(1)}, f32[4,144,1024]{2,1,0:T(8,128)S(1)}, f32[4,144,1024]{2,1,0:T(8,128)S(1)}, f32[4,128,1024]{2,1,0:T(8,128)S(1)}, f3...) custom-call(f32[4,128,1024]{2,1,0:T(8,128)} %b_hbm.1, f32[4,128,1024]{2,1,0:T(8,128)} %r_hbm.1, ...), custom_call_target="tpu_custom_call" | custom-call | tf_op jit(solution)/shard_map/pcg/pallas_call | solution.py:619
  33.3 2.1 %finish.1 = (f32[4,128,1024]{2,1,0:T(8,128)}, f32[4,128,1024]{2,1,0:T(8,128)}) custom-call(f32[4,128,1024]{2,1,0:T(8,128)S(1)} %get-tuple-element.8.bb, f32[4,144,1024]{2,1,0:T(8,128)S(1)} %get-tuple-element.9.zb, f32[4,144,1024]{2,1,0:T(8,128)S(1)} %get-tuple-element.10.vb, f32[4,128,1024]{2,1,0:T(8,128)S(1)} %get-tuple-element.11.wb, ...), custom_call_target="tpu_custom_call" | custom-call | tf_op jit(solution)/shard_map/finish/pallas_call | solution.py:629

commit v2 on v1

--- a/solution.py
+++ b/solution.py
@@ -173,20 +173,20 @@
             sends, _, copy = exchanges(trip)[e]
             pl.when(sends)(copy.wait_send)
 
-    for copy in edge_loads:
-        copy.wait()
+    edge_loads[0].wait()
     for c in range(1, chunks):
         start_loads((1 + c) % chunks)
     for k in range(depth):
         row_s[0, 0, k:k + 1, :] = redge[lay[k], S - 1:S, :]
+    edge_loads[1].wait()
+    for k in range(depth):
         acc = jnp.zeros((S, L), F32)
         for i in range(tiles):
             edge = jnp.broadcast_to(cedge[lay[k], i * S:(i + 1) * S, L - 1:L], (S, L))
             acc = jnp.where(lane == sub + i * S, edge, acc)
         col_s[0, 0, 0, k:k + 1, :] = jnp.sum(acc, axis=0, keepdims=True)
-
     pl.semaphore_wait(barrier, count(near))
-    send_halo(0, (0, 2))
+    send_halo(0, (2, 0))
     hello(0)
     take_halo(0, (2,))
 
@@ -445,7 +445,6 @@
         part = sum_r.at[pl.ds(0, peers - 1)]
         return pltpu.make_async_copy(part, part, sum_sem.at[end])
 
-    heard(0)
     colacc[...] = jnp.zeros_like(colacc)
 
     def wait_middle(c):
@@ -455,6 +454,7 @@
     in_chunks(back_first, before=wait_middle,
               after=lambda c: pl.when(c == chunks - 1)(lambda: send_part(zb, 1, 0, 0)))
     send_part(zb, 1, 1, 1)
+    heard(0)
 
     zero = jnp.zeros((S, L), F32)
 
@@ -480,7 +480,6 @@
         return use
 
     first_sides(zb, 1)
-    heard(1)
     one, two = images(zb, 1, low_tiles, image_first, (zero, zero),
                       after=lambda q: pl.when(q < chunks - 2)(lambda: f2_copy(q + 1).start()))
     f2_copy(0).start()
@@ -489,13 +488,14 @@
     in_chunks(back_second, order=high_last, before=lambda c: f2_copy(c).wait_recv(),
               after=lambda c: pl.when(c == 0)(lambda: send_part(vb, 2, 0, 1)))
     send_part(vb, 2, 1, 0)
-    heard(2)
+    heard(1)
     here = pair_finish(0)
     rho_here, power_here = here[0:1], here[1:2]
     known = power_here > 0.0
     guess = jnp.where(known, jnp.clip(rho_here / jnp.where(known, power_here, 1.0), 0.25, 256.0), 1.0)
     step = jnp.broadcast_to(guess, (S, L))
     first_sides(vb, 2)
+    heard(2)
 
     def image_second(i):
         at, pad = rows_at(i), rows_at(i + 1)

time: 35.5 us -> 35.3 us (level)
  no operation moved by 1% of the time
where the time goes in v2:
time: 35.3 us; the launch traced here: 35.2 us
  Pallas kernels  34.6 us (98%)
  between operations  0.64 us (2%)
    pallas_call x1, Pallas kernels, shards(): pl.pallas_call(functools.partial(kernel, sizes, chunks), out_shape=(vmem(...  32.5 us
    pallas_call x1, Pallas kernels, shards(): pl.pallas_call(functools.partial(finish, 2 * chunks if rows % (2 * chunks...  2.08 us

profile of v2, /device:TPU:1, one launch (start us, length us, event | category | flops | bytes accessed | tf_op | source)
XLA Modules:
  0.0 35.2 jit_solution(3460207266550877005)
XLA Ops:
  0.6 32.5 %pcg.1 = (f32[4,128,1024]{2,1,0:T(8,128)S(1)}, f32[4,144,1024]{2,1,0:T(8,128)S(1)}, f32[4,144,1024]{2,1,0:T(8,128)S(1)}, f32[4,128,1024]{2,1,0:T(8,128)S(1)}, f3...) custom-call(f32[4,128,1024]{2,1,0:T(8,128)} %b_hbm.1, f32[4,128,1024]{2,1,0:T(8,128)} %r_hbm.1, ...), custom_call_target="tpu_custom_call" | custom-call | tf_op jit(solution)/shard_map/pcg/pallas_call | solution.py:619
  33.1 2.1 %finish.1 = (f32[4,128,1024]{2,1,0:T(8,128)}, f32[4,128,1024]{2,1,0:T(8,128)}) custom-call(f32[4,128,1024]{2,1,0:T(8,128)S(1)} %get-tuple-element.8.bb, f32[4,144,1024]{2,1,0:T(8,128)S(1)} %get-tuple-element.9.zb, f32[4,144,1024]{2,1,0:T(8,128)S(1)} %get-tuple-element.10.vb, f32[4,128,1024]{2,1,0:T(8,128)S(1)} %get-tuple-element.11.wb, ...), custom_call_target="tpu_custom_call" | custom-call | tf_op jit(solution)/shard_map/finish/pallas_call | solution.py:629
